TPU v7x, 128 devices: a whole 4x4x4 slice. The times are simulated.
128 devices in a mesh: replica: 2 (over core), fsdp: 16 (over y, x), tensor: 4 (over z).
Axes of the slice: x: 4, y: 4, z: 4, core: 2. Of those that a mesh axis runs over, the one named last changes fastest.
Arguments:
- grads: bfloat16 [2, 2, 4096, 14336], P('replica', None, 'fsdp', 'tensor'), may hold values from -6 to 6
- momentum: bfloat16 [2, 4096, 14336], P(None, 'fsdp', 'tensor'), may hold values from -50 to 50, as said below
- basis: bfloat16 [2, 14336, 512], P(None, 'tensor'), may hold values from -0.046875 to 0.046875
Outputs:
- momentum_new: bfloat16 [2, 4096, 14336], P(None, 'fsdp', 'tensor')
- update: bfloat16 [2, 4096, 14336], P(None, 'fsdp', 'tensor')
- basis_new: bfloat16 [2, 14336, 512], P(None, 'tensor')
Inputs may be any that keep to these rules, and one draw needn't show every extreme that they name: `momentum`: entries are finite.
All inputs are finite; a program needn't handle non-finite values.
Results may differ from a plain program's by a relative error of at most 0.028.
Values may be sent and summed in bfloat16 or wider, within the bound.
A program may use at most 128 MiB of HBM per device.

v0:
```python
import functools
import math
import jax
import jax.numpy as jnp
from jax import lax
from jax.sharding import Mesh
from jax.sharding import PartitionSpec as P

FEATURES = 4096
UNITS = 14336
RANK = 512
FSDP = ("fsdp_0", "fsdp_1")
REPLICA_FSDP_TENSOR = ("replica", "fsdp_0", "fsdp_1", "tensor")
REPLICA_FSDP = ("replica", "fsdp_0", "fsdp_1")
momentum_decay = 0.95


def from_everyone(x, axis):
    size = lax.axis_size(axis)
    return lax.all_to_all(jnp.broadcast_to(x[None], (size, *x.shape)), axis, 0, 0, tiled=True)


def of_everyone(x, axis):
    everything = from_everyone(x, axis)
    return jnp.sum(everything.astype(jnp.float32), axis=0)


def in_blocks(x, dim, size):
    before, after = (x.shape[:dim], x.shape[dim + 1 :])
    return jnp.moveaxis(x.reshape(*before, size, -1, *after), dim, 0)


def piece_ends(length, count):
    unit = 8 if length >= 8 * count else 1
    return [length // unit * k // count * unit for k in range(1, count)]


def own_block(pieces, axes, turns):
    dims = [lax.axis_size(a) for a in axes]
    pieces = pieces.reshape(*dims, *pieces.shape[1:])
    pieces = pieces.transpose(*turns, *range(len(axes), pieces.ndim))
    pieces = pieces.reshape(-1, *pieces.shape[len(axes) :])
    for k in turns:
        pieces = lax.psum_scatter(pieces, axes[k], scatter_dimension=0, tiled=True)
    return pieces[0]


def spread_scatter(x, axes, dim):
    pieces = in_blocks(x, dim, lax.axis_size(axes))
    cut = max(range(1, max(2, pieces.ndim - 1)), key=lambda d: pieces.shape[d])
    count, done = (len(axes), [])
    for initial, section in enumerate(
        jnp.split(pieces, piece_ends(pieces.shape[cut], count), axis=cut)
    ):
        if section.size:
            turns = [(initial + k) % count for k in range(count)]
            done.append(own_block(section, axes, turns))
    return jnp.concatenate(done, axis=cut - 1)


def over_axes(x, axes):
    return functools.reduce(lax.psum, axes, x)


def total_of_pieces(x, axis):
    return lax.all_gather(x, axis).astype(jnp.float32).sum(0)


def orthonormal(projected, factor):

    def solve_one(lower_mat, rows_mat):
        return jax.scipy.linalg.solve_triangular(lower_mat, rows_mat.T, lower=True).T

    return jax.vmap(solve_one)(factor, projected).astype(jnp.bfloat16)


def power_step(total_grad, moment, right):
    blended = (moment.astype(jnp.float32) + total_grad).astype(jnp.bfloat16)
    partial_value = jnp.einsum("wmc,wcr->wmr", blended, right, preferred_element_type=jnp.float32)
    projected = of_everyone(partial_value.astype(jnp.bfloat16), "tensor").astype(jnp.float32)
    gram_local = jnp.einsum(
        "wmr,wms->wrs", projected, projected, preferred_element_type=jnp.float32
    )
    gram_matrix = lax.psum(gram_local.astype(jnp.bfloat16), FSDP).astype(jnp.float32)
    factor = jnp.linalg.cholesky(gram_matrix)
    left_basis = orthonormal(projected, factor)
    half = blended.shape[2] // lax.axis_size("replica")
    offset = lax.axis_index("replica") * half
    kept_half = half // lax.axis_size(FSDP)
    columns = lax.dynamic_slice_in_dim(blended, offset, kept_half * lax.axis_size(FSDP), 2)
    back_piece = spread_scatter(
        jnp.einsum("wmc,wmr->cwr", columns, left_basis, preferred_element_type=jnp.float32).astype(
            jnp.bfloat16
        ),
        FSDP,
        0,
    ).astype(jnp.float32)
    squares = over_axes(jnp.sum(back_piece * back_piece, axis=0), REPLICA_FSDP_TENSOR)
    back_b = back_piece.astype(jnp.bfloat16)
    right_rows = lax.all_gather(back_b, REPLICA_FSDP, axis=0, tiled=True)
    inverse = 1.0 / (jnp.sqrt(squares) + 1e-06)
    normed = (right_rows.astype(jnp.float32) * inverse[None, :, :]).astype(jnp.bfloat16)
    feedback = jnp.einsum(
        "wmr,cwr->wmc", left_basis, right_rows, preferred_element_type=jnp.float32
    )
    momentum_new = (blended.astype(jnp.float32) - (1.0 - momentum_decay) * feedback).astype(
        jnp.bfloat16
    )
    scale = math.sqrt(FEATURES * UNITS / RANK)
    update = (
        scale * jnp.einsum("wmr,cwr->wmc", left_basis, normed, preferred_element_type=jnp.float32)
    ).astype(jnp.bfloat16)
    basis_new = jnp.transpose(normed, (1, 0, 2))
    return (momentum_new, update, basis_new)


def summed_grads(grads):
    return total_of_pieces(grads[0].astype(jnp.float32).astype(jnp.bfloat16), "replica").astype(
        jnp.float32
    )


def shards(grads, momentum, basis):
    return power_step(summed_grads(grads), momentum, basis)


def solution(mesh):
    torus = Mesh(
        mesh.devices.reshape(mesh.shape["replica"], 4, 4, mesh.shape["tensor"]),
        ("replica", "fsdp_0", "fsdp_1", "tensor"),
    )
    return jax.shard_map(
        shards,
        mesh=torus,
        in_specs=(
            P("replica", None, FSDP, "tensor"),
            P(None, FSDP, "tensor"),
            P(None, "tensor", None),
        ),
        out_specs=(P(None, FSDP, "tensor"), P(None, FSDP, "tensor"), P(None, "tensor", None)),
        check_vma=False,
    )
```

profile of v0, /device:TPU:1, one launch (start us, length us, event | category | flops | bytes accessed | tf_op | source)
XLA Modules:
  0.0 627.0 jit_solution(4297394936807727248)
XLA Ops:
  7.9 26.3 %all-gather.3.cloned.1.call-done = bf16[2,2,256,3584]{3,2,1,0:T(8,128)(2,1)} async-done(((bf16[1,2,256,3584]{3,2,1,0:T(8,128)(2,1)}), bf16[2,2,256,3584]{3,2,1,0:T(8,128)(2,1)}) %all-gather.3.cloned.1.call-update) | async-done | bytes 7340048 | tf_op jit(solution)/shard_map/all_gather | solution.py:66
  34.3 5.3 convert_reduce_fusion
  40.7 6.5 %convolution_convert_fusion.2 = bf16[2,256,512]{2,1,0:T(8,128)(2,1)S(1)} fusion(bf16[2,256,3584]{2,1,0:T(8,128)(2,1)S(1)} %add_convert_fusion, bf16[2,3584,512]{2,1,0:T(8,128)(2,1)} %param.5), kind=kOutput, calls=%fused_computation.16 | convolution fusion | flops 1879310336 | bytes 11534336 | tf_op jit(solution)/shard_map/wmc,wcr->wmr/dot_general | solution.py:79
  47.4 30.0 %all_to_all.5 = bf16[4,2,256,512]{3,2,1,0:T(8,128)(2,1)S(1)} all-to-all(bf16[4,2,256,512]{3,2,1,0:T(8,128)(2,1)S(1)} %broadcast_in_dim.4), channel_id=1, replica_groups=mesh['replica'=2,'fsdp_0'=4,'fsdp_1'=4,'tensor'=4] {'tensor'}, dimensions={0} | all-to-all | bytes 4194304 | tf_op jit(solution)/shard_map/all_to_all | solution.py:20
  77.7 1.5 fusion.38
  79.9 1.3 copy.72
  81.2 83.7 %all-reduce.3.cloned.1.call-done = bf16[2,512,512]{1,2,0:T(8,128)(2,1)} async-done(((bf16[2,512,512]{1,2,0:T(8,128)(2,1)}), bf16[2,512,512]{1,2,0:T(8,128)(2,1)}) %all-reduce.3.cloned.1.call-update) | async-done | bytes 1048592 | tf_op jit(solution)/shard_map/psum | solution.py:84
  164.9 1.6 copy.64
  166.8 1.3 copy-done.3
  168.1 23.5 %custom-call.35 = f32[2,128,128]{2,1,0:T(8,128)S(1)} custom-call(f32[2,128,128]{2,1,0:T(8,128)S(1)} %cholesky.274), custom_call_target="Cholesky" | custom-call | tf_op jit(solution)/shard_map/jit(cholesky)/cholesky | solution.py:85
  191.6 19.7 %custom-call.36 = f32[2,1,128,128]{2,3,1,0:T(8,128)S(1)} custom-call(f32[2,1,128,128]{3,2,1,0:T(8,128)S(1)} %select_bitcast_fusion.2), custom_call_target="InvertDiagBlocksLowerTriangular" | custom-call | tf_op jit(solution)/shard_map/jit(cholesky)/cholesky | solution.py:85
  211.6 1.5 constant_dynamic-update-slice_fusion.3
  213.1 1.5 convolution_subtract_fusion
  214.6 23.5 %custom-call.37 = f32[2,128,128]{2,1,0:T(8,128)S(1)} custom-call(f32[2,128,128]{2,1,0:T(8,128)S(1)} %cholesky.278), custom_call_target="Cholesky" | custom-call | tf_op jit(solution)/shard_map/jit(cholesky)/cholesky | solution.py:85
  238.1 19.8 %custom-call.38 = f32[2,1,128,128]{2,3,1,0:T(8,128)S(1)} custom-call(f32[2,1,128,128]{3,2,1,0:T(8,128)S(1)} %get-tuple-element.30), custom_call_target="InvertDiagBlocksLowerTriangular" | custom-call | tf_op jit(solution)/shard_map/jit(cholesky)/cholesky | solution.py:85
  258.3 1.6 convolution_subtract_fusion.3
  259.9 23.5 %custom-call.39 = f32[2,128,128]{2,1,0:T(8,128)S(1)} custom-call(f32[2,128,128]{2,1,0:T(8,128)S(1)} %cholesky.283), custom_call_target="Cholesky" | custom-call | tf_op jit(solution)/shard_map/jit(cholesky)/cholesky | solution.py:85
  283.4 19.7 %custom-call.40 = f32[2,1,128,128]{2,3,1,0:T(8,128)S(1)} custom-call(f32[2,1,128,128]{3,2,1,0:T(8,128)S(1)} %get-tuple-element.28), custom_call_target="InvertDiagBlocksLowerTriangular" | custom-call | tf_op jit(solution)/shard_map/jit(cholesky)/cholesky | solution.py:85
  303.4 1.5 convolution_subtract_fusion.5
  304.9 23.7 %custom-call.41 = f32[2,128,128]{2,1,0:T(8,128)S(1)} custom-call(f32[2,128,128]{2,1,0:T(8,128)S(1)} %convolution_subtract_fusion.5), custom_call_target="Cholesky" | custom-call | tf_op jit(solution)/shard_map/jit(cholesky)/cholesky | solution.py:85
  328.9 1.7 select_select_fusion
  330.7 14.5 %while.1 = (s32[]{:T(128)}, f32[2,512,512]{2,1,0:T(8,128)}, s32[4,2]{0,1:T(2,128)S(1)}, f32[4,2,128,128]{3,2,0,1:T(8,128)}, s32[]{:T(128)}) while((s32[]{:T(128)}, f32[2,512,512]{2,1,0:T(8,128)}, s32[4,2]{0,1:T(2,128)S(1)}, f32[4,2,128,128]{3,2,0,1:T(8,128)}, s32[]{:T(128)}) %tuple.36), condition=%wide.while_cond, body=%wide.while_body.sunk | while | flops 2 | bytes 263277 | solution.py:72
  331.4 3.0 bitcast_dynamic-update-slice_fusion.2
  335.0 3.0 bitcast_dynamic-update-slice_fusion.2
  338.6 3.0 bitcast_dynamic-update-slice_fusion.2
  342.3 2.9 bitcast_dynamic-update-slice_fusion.2
  345.2 79.4 %custom-call.42 = f32[2,4,128,128]{2,3,1,0:T(8,128)S(1)} custom-call(f32[2,4,128,128]{3,2,1,0:T(8,128)} %bitcast.91), custom_call_target="InvertDiagBlocksLowerTriangular" | custom-call | tf_op jit(solution)/shard_map/vmap(jit(_solve_triangular))/triangular_solve | solution.py:72
  425.1 1.3 convolution_subtract_fusion.2
  426.8 1.6 convolution_subtract_fusion.1
  428.8 1.7 convolution_subtract_fusion.4
  430.9 3.0 fusion.1
  433.9 5.9 copy.77
  439.8 2.4 fusion.34
  442.3 1.5 copy.79
  443.8 1.5 copy.95
  445.3 26.8 %reduce-scatter.9.cloned.1.call-done = bf16[4,56,2,512]{3,1,2,0:T(8,128)(2,1)} async-done(((bf16[16,56,2,512]{3,1,2,0:T(8,128)(2,1)}), bf16[4,56,2,512]{3,1,2,0:T(8,128)(2,1)}) %reduce-scatter.9.cloned.1.call-update) | async-done | bytes 458768 | tf_op jit(solution)/shard_map/reduce_scatter | solution.py:44
  472.2 30.1 %reduce-scatter.5.cloned.1.call-done = bf16[4,56,2,512]{3,1,2,0:T(8,128)(2,1)} async-done(((bf16[16,56,2,512]{3,1,2,0:T(8,128)(2,1)}), bf16[4,56,2,512]{3,1,2,0:T(8,128)(2,1)}) %reduce-scatter.5.cloned.1.call-update) | async-done | bytes 458768 | tf_op jit(solution)/shard_map/reduce_scatter | solution.py:44
  502.4 21.0 %reduce-scatter.11.cloned.1.call-done = bf16[1,56,2,512]{3,1,2,0:T(8,128)(2,1)} async-done(((bf16[4,56,2,512]{3,1,2,0:T(8,128)(2,1)}), bf16[1,56,2,512]{3,1,2,0:T(8,128)(2,1)}) %reduce-scatter.11.cloned.1.call-update) | async-done | bytes 114704 | tf_op jit(solution)/shard_map/reduce_scatter | solution.py:44
  523.4 23.3 %reduce-scatter.7.cloned.1.call-done = bf16[1,56,2,512]{3,1,2,0:T(8,128)(2,1)} async-done(((bf16[4,56,2,512]{3,1,2,0:T(8,128)(2,1)}), bf16[1,56,2,512]{3,1,2,0:T(8,128)(2,1)}) %reduce-scatter.7.cloned.1.call-update) | async-done | bytes 114704 | tf_op jit(solution)/shard_map/reduce_scatter | solution.py:44
  546.8 1.7 pad_maximum_fusion.1
  549.5 5.1 psum.36
  554.6 8.4 %psum.37 = f32[2,512]{1,0:T(2,128)S(1)} all-reduce(f32[2,512]{1,0:T(2,128)S(1)} %psum.36), channel_id=1, replica_groups=mesh['replica'=2,'fsdp_0'=4,'fsdp_1'=4,'tensor'=4] {'fsdp_0'}, use_global_device_ids=true, to_apply=%region_17.18 | all-reduce | flops 1024 | bytes 8192 | tf_op jit(solution)/shard_map/psum | solution.py:62
  563.0 6.5 %psum.38 = f32[2,512]{1,0:T(2,128)S(1)} all-reduce(f32[2,512]{1,0:T(2,128)S(1)} %psum.37), channel_id=1, replica_groups=mesh['replica'=2,'fsdp_0'=4,'fsdp_1'=4,'tensor'=4] {'fsdp_1'}, use_global_device_ids=true, to_apply=%region_18.19 | all-reduce | flops 1024 | bytes 8192 | tf_op jit(solution)/shard_map/psum | solution.py:62
  569.5 9.2 %psum.39 = f32[2,512]{1,0:T(2,128)S(1)} all-reduce(f32[2,512]{1,0:T(2,128)S(1)} %psum.38), channel_id=1, replica_groups=mesh['replica'=2,'fsdp_0'=4,'fsdp_1'=4,'tensor'=4] {'tensor'}, use_global_device_ids=true, to_apply=%region_19.20 | all-reduce | flops 1024 | bytes 8192 | tf_op jit(solution)/shard_map/psum | solution.py:62
  578.8 24.0 %all-gather.5.cloned.1.call-done = bf16[3584,2,512]{2,0,1:T(8,128)(2,1)} async-done(((bf16[112,2,512]{2,0,1:T(8,128)(2,1)}), bf16[3584,2,512]{2,0,1:T(8,128)(2,1)}) %all-gather.5.cloned.1.call-update) | async-done | bytes 7340048 | tf_op jit(solution)/shard_map/all_gather | solution.py:100
  602.8 8.3 %subtract_convert_fusion = bf16[2,256,3584]{2,1,0:T(8,128)(2,1)} fusion(bf16[2,256,3584]{2,1,0:T(8,128)(2,1)} %copy-done, bf16[3584,2,512]{2,0,1:T(8,128)(2,1)} %all-gather.5.cloned.1.call-done, bf16[2,128,256]{2,1,0:T(8,128)(2,1)S(1)} %convolution_convert_fusion.3, bf16[2,128,256]{2,1,0:T(8,128)(2,1)S(1)} %get-tuple-element.34, ...), kind=kOutput, calls=%fused_computation.5 | convolution fusion | flops 1888485376 | bytes 15204352 | tf_op jit(solution)/shard_map/wmr,cwr->wmc/dot_general | solution.py:103
  611.1 4.3 multiply_convert_fusion.1
  615.4 4.5 fusion
  (64 shorter events, 10.4 us)
Async XLA Ops:
  7.2 27.1 %all-gather.3.cloned.1.call-start = ((), (), s32[]{:S(2)}) async-start(), calls=%async_computation.5 | async-start | bytes 11010048 | tf_op jit(solution)/shard_map/all_gather | solution.py:66
  7.9 157.0 %all-reduce.3.cloned.1.call-start = ((), (), s32[]{:S(2)}) async-start(), calls=%async_computation.6 | async-start | bytes 2097152 | tf_op jit(solution)/shard_map/psum | solution.py:84
  34.3 5.3 copy-start.6
  40.7 6.5 %copy-start = (bf16[2,256,3584]{2,1,0:T(8,128)(2,1)}, bf16[2,256,3584]{2,1,0:T(8,128)(2,1)S(1)}, u32[]{:S(2)}) copy-start(bf16[2,256,3584]{2,1,0:T(8,128)(2,1)S(1)} %add_convert_fusion) | copy-start | bytes 11010052
  79.1 393.0 %reduce-scatter.9.cloned.1.call-start = ((), (), s32[]{:S(2)}) async-start(), calls=%async_computation.9 | async-start | bytes 2293760 | tf_op jit(solution)/shard_map/reduce_scatter | solution.py:44
  164.9 1.6 copy-start.4
  166.8 1.3 copy-start.3
  328.9 95.7 %copy-start.5 = (f32[2,256,512]{1,2,0:T(8,128)S(1)}, f32[2,256,512]{1,2,0:T(8,128)}, u32[]{:S(2)}) copy-start(f32[2,256,512]{1,2,0:T(8,128)} %copy.72) | copy-start | bytes 3145732
  426.8 4.1 copy-start.1
  443.7 58.6 %reduce-scatter.5.cloned.1.call-start = ((), (), s32[]{:S(2)}) async-start(), calls=%async_computation.7 | async-start | bytes 2293760 | tf_op jit(solution)/shard_map/reduce_scatter | solution.py:44
  445.3 78.1 %reduce-scatter.11.cloned.1.call-start = ((), (), s32[]{:S(2)}) async-start(), calls=%async_computation.10 | async-start | bytes 573440 | tf_op jit(solution)/shard_map/reduce_scatter | solution.py:44
  472.2 74.6 %reduce-scatter.7.cloned.1.call-start = ((), (), s32[]{:S(2)}) async-start(), calls=%async_computation.8 | async-start | bytes 573440 | tf_op jit(solution)/shard_map/reduce_scatter | solution.py:44
  502.4 100.4 %all-gather.5.cloned.1.call-start = ((), (), s32[]{:S(2)}) async-start(), calls=%async_computation.11 | async-start | bytes 7569408 | tf_op jit(solution)/shard_map/all_gather | solution.py:100
  602.8 8.3 %copy-start.2 = (bf16[3584,2,512]{2,0,1:T(8,128)(2,1)S(1)}, bf16[3584,2,512]{2,0,1:T(8,128)(2,1)}, u32[]{:S(2)}) copy-start(bf16[3584,2,512]{2,0,1:T(8,128)(2,1)} %all-gather.5.cloned.1.call-done) | copy-start | bytes 22020100
Sparse Core Ops, SparseCore 0:
  9.6 24.6 all-gather.2
  79.3 85.5 all-reduce.2
  443.9 28.2 reduce-scatter.8
  475.0 27.3 reduce-scatter.4
  504.6 18.7 reduce-scatter.10
  525.7 21.0 reduce-scatter.6
  549.6 53.1 all-gather.4
where the time goes:
time: 632 us; the launch traced here: 627 us
  other arithmetic  249 us (39%)
  waiting for transfers between devices  236 us (37%)
  blocking collectives  59.2 us (9%)
  matrix products  36.4 us (6%)
  local copies, waits for them, and re-layouts  30.5 us (5%)
  between operations  14.8 us (2%)
    another operation x16, other arithmetic, power_step(): factor = jnp.linalg.cholesky(gram_matrix)  154 us
    reduce_scatter x4, waiting for transfers between devices, own_block(): pieces = lax.psum_scatter(pieces, axes[k], scatter_dimension=0, tiled=True)  101 us
    psum x1, waiting for transfers between devices, power_step(): lax.psum(gram_local.astype(jnp.bfloat16), FSDP).astype(jnp.float32)  83.7 us
    another operation x4, other arithmetic, solve_one(): jax.scipy.linalg.solve_triangular(lower_mat, rows_mat.T, lower=True)  81.2 us
    all_to_all x1, blocking collectives, from_everyone(): lax.all_to_all(jnp.broadcast_to(x[None], (size, *x.shape)), axis, 0, 0, t...  30 us
    psum x4, blocking collectives, over_axes(): return functools.reduce(lax.psum, axes, x)  29.3 us
    all_gather x1, waiting for transfers between devices, total_of_pieces(): return lax.all_gather(x, axis).astype(jnp.float32).sum(0)  26.3 us
    all_gather x1, waiting for transfers between devices, power_step(): right_rows = lax.all_gather(back_b, REPLICA_FSDP, axis=0, tiled=True)  24 us
  transfers between devices with their start and end apart: 7, of which 7 were waited for; matrix products, arithmetic and copies ran while one was open for 1% of the time, Pallas kernels for 0%

commit v1 on v0

--- a/solution.py
+++ b/solution.py
@@ -13,6 +13,11 @@
 REPLICA_FSDP_TENSOR = ("replica", "fsdp_0", "fsdp_1", "tensor")
 REPLICA_FSDP = ("replica", "fsdp_0", "fsdp_1")
 momentum_decay = 0.95
+
+
+def by_each_axis(array, axis_one, axis_two):
+    middle = lax.psum(array, axis_one)
+    return lax.psum(middle, axis_two)
 
 
 def from_everyone(x, axis):
@@ -81,7 +86,9 @@
     gram_local = jnp.einsum(
         "wmr,wms->wrs", projected, projected, preferred_element_type=jnp.float32
     )
-    gram_matrix = lax.psum(gram_local.astype(jnp.bfloat16), FSDP).astype(jnp.float32)
+    gram_matrix = by_each_axis(gram_local.astype(jnp.bfloat16), "fsdp_0", "fsdp_1").astype(
+        jnp.float32
+    )
     factor = jnp.linalg.cholesky(gram_matrix)
     left_basis = orthonormal(projected, factor)
     half = blended.shape[2] // lax.axis_size("replica")

time: 632 us -> 642 us (1.016)
  waiting for transfers between devices: 236 us -> 246 us
    psum x1 -> x2, waiting for transfers between devices: 83.7 us -> 91.6 us  [the longest x1 47.3 us: by_each_axis(): return lax.psum(middle, axis_two)]
  transfers between devices with their start and end apart: 7 -> 8, of which waited for: 7 -> 8; matrix products, arithmetic and copies ran while one was open for 1% -> 1% of each run, Pallas kernels for 0% -> 0%
where the time goes in v1:
time: 642 us; the launch traced here: 637 us
  other arithmetic  249 us (39%)
  waiting for transfers between devices  246 us (38%)
  blocking collectives  59.2 us (9%)
  matrix products  36.4 us (6%)
  local copies, waits for them, and re-layouts  30.5 us (5%)
  between operations  14.8 us (2%)
    another operation x16, other arithmetic, power_step(): factor = jnp.linalg.cholesky(gram_matrix)  154 us
    reduce_scatter x4, waiting for transfers between devices, own_block(): pieces = lax.psum_scatter(pieces, axes[k], scatter_dimension=0, tiled=True)  103 us
    another operation x4, other arithmetic, solve_one(): jax.scipy.linalg.solve_triangular(lower_mat, rows_mat.T, lower=True)  81.2 us
    psum x1, waiting for transfers between devices, by_each_axis(): return lax.psum(middle, axis_two)  47.3 us
    psum x1, waiting for transfers between devices, by_each_axis(): middle = lax.psum(array, axis_one)  44.3 us
    all_to_all x1, blocking collectives, from_everyone(): lax.all_to_all(jnp.broadcast_to(x[None], (size, *x.shape)), axis, 0, 0, t...  30 us
    psum x4, blocking collectives, over_axes(): return functools.reduce(lax.psum, axes, x)  29.2 us
    all_gather x1, waiting for transfers between devices, total_of_pieces(): return lax.all_gather(x, axis).astype(jnp.float32).sum(0)  26.3 us
  transfers between devices with their start and end apart: 8, of which 8 were waited for; matrix products, arithmetic and copies ran while one was open for 1% of the time, Pallas kernels for 0%

profile of v1, /device:TPU:1, one launch (start us, length us, event | category | flops | bytes accessed | tf_op | source)
XLA Modules:
  0.0 637.2 jit_solution(10419069845722586621)
XLA Ops:
  7.9 26.3 %all-gather.3.cloned.1.call-done = bf16[2,2,256,3584]{3,2,1,0:T(8,128)(2,1)} async-done(((bf16[1,2,256,3584]{3,2,1,0:T(8,128)(2,1)}), bf16[2,2,256,3584]{3,2,1,0:T(8,128)(2,1)}) %all-gather.3.cloned.1.call-update) | async-done | bytes 7340048 | tf_op jit(solution)/shard_map/all_gather | solution.py:71
  34.3 5.3 convert_reduce_fusion
  40.7 6.5 %convolution_convert_fusion.2 = bf16[2,256,512]{2,1,0:T(8,128)(2,1)S(1)} fusion(bf16[2,256,3584]{2,1,0:T(8,128)(2,1)S(1)} %add_convert_fusion, bf16[2,3584,512]{2,1,0:T(8,128)(2,1)} %param.5), kind=kOutput, calls=%fused_computation.16 | convolution fusion | flops 1879310336 | bytes 11534336 | tf_op jit(solution)/shard_map/wmc,wcr->wmr/dot_general | solution.py:84
  47.4 30.0 %all_to_all.5 = bf16[4,2,256,512]{3,2,1,0:T(8,128)(2,1)S(1)} all-to-all(bf16[4,2,256,512]{3,2,1,0:T(8,128)(2,1)S(1)} %broadcast_in_dim.4), channel_id=1, replica_groups=mesh['replica'=2,'fsdp_0'=4,'fsdp_1'=4,'tensor'=4] {'tensor'}, dimensions={0} | all-to-all | bytes 4194304 | tf_op jit(solution)/shard_map/all_to_all | solution.py:25
  77.7 1.5 fusion.38
  79.2 44.3 %all-reduce.4.cloned.1.call-done = bf16[2,512,512]{1,2,0:T(8,128)(2,1)} async-done(((bf16[2,512,512]{1,2,0:T(8,128)(2,1)}), bf16[2,512,512]{1,2,0:T(8,128)(2,1)}) %all-reduce.4.cloned.1.call-update) | async-done | bytes 1048592 | tf_op jit(solution)/shard_map/psum | solution.py:19
  124.3 1.3 copy.72
  125.6 47.3 %all-reduce.6.cloned.1.call-done = bf16[2,512,512]{1,2,0:T(8,128)(2,1)} async-done(((bf16[2,512,512]{1,2,0:T(8,128)(2,1)}), bf16[2,512,512]{1,2,0:T(8,128)(2,1)}) %all-reduce.6.cloned.1.call-update) | async-done | bytes 1048592 | tf_op jit(solution)/shard_map/psum | solution.py:20
  172.9 1.6 copy.64
  174.8 1.3 copy-done.3
  176.2 23.5 %custom-call.35 = f32[2,128,128]{2,1,0:T(8,128)S(1)} custom-call(f32[2,128,128]{2,1,0:T(8,128)S(1)} %cholesky.274), custom_call_target="Cholesky" | custom-call | tf_op jit(solution)/shard_map/jit(cholesky)/cholesky | solution.py:92
  199.7 19.7 %custom-call.36 = f32[2,1,128,128]{2,3,1,0:T(8,128)S(1)} custom-call(f32[2,1,128,128]{3,2,1,0:T(8,128)S(1)} %select_bitcast_fusion.2), custom_call_target="InvertDiagBlocksLowerTriangular" | custom-call | tf_op jit(solution)/shard_map/jit(cholesky)/cholesky | solution.py:92
  219.6 1.5 constant_dynamic-update-slice_fusion.3
  221.1 1.5 convolution_subtract_fusion
  222.6 23.5 %custom-call.37 = f32[2,128,128]{2,1,0:T(8,128)S(1)} custom-call(f32[2,128,128]{2,1,0:T(8,128)S(1)} %cholesky.278), custom_call_target="Cholesky" | custom-call | tf_op jit(solution)/shard_map/jit(cholesky)/cholesky | solution.py:92
  246.1 19.8 %custom-call.38 = f32[2,1,128,128]{2,3,1,0:T(8,128)S(1)} custom-call(f32[2,1,128,128]{3,2,1,0:T(8,128)S(1)} %get-tuple-element.30), custom_call_target="InvertDiagBlocksLowerTriangular" | custom-call | tf_op jit(solution)/shard_map/jit(cholesky)/cholesky | solution.py:92
  266.4 1.6 convolution_subtract_fusion.3
  267.9 23.5 %custom-call.39 = f32[2,128,128]{2,1,0:T(8,128)S(1)} custom-call(f32[2,128,128]{2,1,0:T(8,128)S(1)} %cholesky.283), custom_call_target="Cholesky" | custom-call | tf_op jit(solution)/shard_map/jit(cholesky)/cholesky | solution.py:92
  291.4 19.7 %custom-call.40 = f32[2,1,128,128]{2,3,1,0:T(8,128)S(1)} custom-call(f32[2,1,128,128]{3,2,1,0:T(8,128)S(1)} %get-tuple-element.28), custom_call_target="InvertDiagBlocksLowerTriangular" | custom-call | tf_op jit(solution)/shard_map/jit(cholesky)/cholesky | solution.py:92
  311.4 1.5 convolution_subtract_fusion.5
  312.9 23.7 %custom-call.41 = f32[2,128,128]{2,1,0:T(8,128)S(1)} custom-call(f32[2,128,128]{2,1,0:T(8,128)S(1)} %convolution_subtract_fusion.5), custom_call_target="Cholesky" | custom-call | tf_op jit(solution)/shard_map/jit(cholesky)/cholesky | solution.py:92
  337.0 1.7 select_select_fusion
  338.7 14.5 %while.1 = (s32[]{:T(128)}, f32[2,512,512]{2,1,0:T(8,128)}, s32[4,2]{0,1:T(2,128)S(1)}, f32[4,2,128,128]{3,2,0,1:T(8,128)}, s32[]{:T(128)}) while((s32[]{:T(128)}, f32[2,512,512]{2,1,0:T(8,128)}, s32[4,2]{0,1:T(2,128)S(1)}, f32[4,2,128,128]{3,2,0,1:T(8,128)}, s32[]{:T(128)}) %tuple.36), condition=%wide.while_cond, body=%wide.while_body.sunk | while | flops 2 | bytes 263277 | solution.py:77
  339.4 3.0 bitcast_dynamic-update-slice_fusion.2
  343.0 3.0 bitcast_dynamic-update-slice_fusion.2
  346.7 3.0 bitcast_dynamic-update-slice_fusion.2
  350.3 2.9 bitcast_dynamic-update-slice_fusion.2
  353.3 79.4 %custom-call.42 = f32[2,4,128,128]{2,3,1,0:T(8,128)S(1)} custom-call(f32[2,4,128,128]{3,2,1,0:T(8,128)} %bitcast.91), custom_call_target="InvertDiagBlocksLowerTriangular" | custom-call | tf_op jit(solution)/shard_map/vmap(jit(_solve_triangular))/triangular_solve | solution.py:77
  434.9 1.6 convolution_subtract_fusion.1
  436.9 1.7 convolution_subtract_fusion.4
  439.0 3.0 fusion.1
  441.9 5.9 copy.77
  447.9 2.4 fusion.34
  450.3 1.5 copy.79
  451.8 1.5 copy.95
  453.4 28.8 %reduce-scatter.9.cloned.1.call-done = bf16[4,56,2,512]{3,1,2,0:T(8,128)(2,1)} async-done(((bf16[16,56,2,512]{3,1,2,0:T(8,128)(2,1)}), bf16[4,56,2,512]{3,1,2,0:T(8,128)(2,1)}) %reduce-scatter.9.cloned.1.call-update) | async-done | bytes 458768 | tf_op jit(solution)/shard_map/reduce_scatter | solution.py:49
  482.2 30.1 %reduce-scatter.5.cloned.1.call-done = bf16[4,56,2,512]{3,1,2,0:T(8,128)(2,1)} async-done(((bf16[16,56,2,512]{3,1,2,0:T(8,128)(2,1)}), bf16[4,56,2,512]{3,1,2,0:T(8,128)(2,1)}) %reduce-scatter.5.cloned.1.call-update) | async-done | bytes 458768 | tf_op jit(solution)/shard_map/reduce_scatter | solution.py:49
  512.4 21.0 %reduce-scatter.11.cloned.1.call-done = bf16[1,56,2,512]{3,1,2,0:T(8,128)(2,1)} async-done(((bf16[4,56,2,512]{3,1,2,0:T(8,128)(2,1)}), bf16[1,56,2,512]{3,1,2,0:T(8,128)(2,1)}) %reduce-scatter.11.cloned.1.call-update) | async-done | bytes 114704 | tf_op jit(solution)/shard_map/reduce_scatter | solution.py:49
  533.5 23.5 %reduce-scatter.7.cloned.1.call-done = bf16[1,56,2,512]{3,1,2,0:T(8,128)(2,1)} async-done(((bf16[4,56,2,512]{3,1,2,0:T(8,128)(2,1)}), bf16[1,56,2,512]{3,1,2,0:T(8,128)(2,1)}) %reduce-scatter.7.cloned.1.call-update) | async-done | bytes 114704 | tf_op jit(solution)/shard_map/reduce_scatter | solution.py:49
  556.9 1.7 pad_maximum_fusion.1
  559.6 5.1 psum.44
  564.8 8.4 %psum.45 = f32[2,512]{1,0:T(2,128)S(1)} all-reduce(f32[2,512]{1,0:T(2,128)S(1)} %psum.44), channel_id=1, replica_groups=mesh['replica'=2,'fsdp_0'=4,'fsdp_1'=4,'tensor'=4] {'fsdp_0'}, use_global_device_ids=true, to_apply=%region_18.19 | all-reduce | flops 1024 | bytes 8192 | tf_op jit(solution)/shard_map/psum | solution.py:67
  573.2 6.4 %psum.46 = f32[2,512]{1,0:T(2,128)S(1)} all-reduce(f32[2,512]{1,0:T(2,128)S(1)} %psum.45), channel_id=1, replica_groups=mesh['replica'=2,'fsdp_0'=4,'fsdp_1'=4,'tensor'=4] {'fsdp_1'}, use_global_device_ids=true, to_apply=%region_19.20 | all-reduce | flops 1024 | bytes 8192 | tf_op jit(solution)/shard_map/psum | solution.py:67
  579.6 9.2 %psum.47 = f32[2,512]{1,0:T(2,128)S(1)} all-reduce(f32[2,512]{1,0:T(2,128)S(1)} %psum.46), channel_id=1, replica_groups=mesh['replica'=2,'fsdp_0'=4,'fsdp_1'=4,'tensor'=4] {'tensor'}, use_global_device_ids=true, to_apply=%region_20.21 | all-reduce | flops 1024 | bytes 8192 | tf_op jit(solution)/shard_map/psum | solution.py:67
  588.9 24.0 %all-gather.5.cloned.1.call-done = bf16[3584,2,512]{2,0,1:T(8,128)(2,1)} async-done(((bf16[112,2,512]{2,0,1:T(8,128)(2,1)}), bf16[3584,2,512]{2,0,1:T(8,128)(2,1)}) %all-gather.5.cloned.1.call-update) | async-done | bytes 7340048 | tf_op jit(solution)/shard_map/all_gather | solution.py:107
  612.9 8.3 %subtract_convert_fusion = bf16[2,256,3584]{2,1,0:T(8,128)(2,1)} fusion(bf16[2,256,3584]{2,1,0:T(8,128)(2,1)} %copy-done, bf16[3584,2,512]{2,0,1:T(8,128)(2,1)} %all-gather.5.cloned.1.call-done, bf16[2,128,256]{2,1,0:T(8,128)(2,1)S(1)} %convolution_convert_fusion.3, bf16[2,128,256]{2,1,0:T(8,128)(2,1)S(1)} %get-tuple-element.34, ...), kind=kOutput, calls=%fused_computation.5 | convolution fusion | flops 1888485376 | bytes 15204352 | tf_op jit(solution)/shard_map/wmr,cwr->wmc/dot_general | solution.py:110
  621.3 4.3 multiply_convert_fusion.1
  625.5 4.5 fusion
  (67 shorter events, 11.7 us)
Async XLA Ops:
  7.2 27.1 %all-gather.3.cloned.1.call-start = ((), (), s32[]{:S(2)}) async-start(), calls=%async_computation.5 | async-start | bytes 11010048 | tf_op jit(solution)/shard_map/all_gather | solution.py:71
  7.9 115.6 %all-reduce.4.cloned.1.call-start = ((), (), s32[]{:S(2)}) async-start(), calls=%async_computation.6 | async-start | bytes 2097152 | tf_op jit(solution)/shard_map/psum | solution.py:19
  34.3 5.3 copy-start.6
  40.7 6.5 %copy-start = (bf16[2,256,3584]{2,1,0:T(8,128)(2,1)}, bf16[2,256,3584]{2,1,0:T(8,128)(2,1)S(1)}, u32[]{:S(2)}) copy-start(bf16[2,256,3584]{2,1,0:T(8,128)(2,1)S(1)} %add_convert_fusion) | copy-start | bytes 11010052
  79.1 93.8 %all-reduce.6.cloned.1.call-start = ((), (), s32[]{:S(2)}) async-start(), calls=%async_computation.7 | async-start | bytes 2097152 | tf_op jit(solution)/shard_map/psum | solution.py:20
  123.5 358.6 %reduce-scatter.9.cloned.1.call-start = ((), (), s32[]{:S(2)}) async-start(), calls=%async_computation.10 | async-start | bytes 2293760 | tf_op jit(solution)/shard_map/reduce_scatter | solution.py:49
  172.9 1.6 copy-start.4
  174.8 1.3 copy-start.3
  337.0 95.7 %copy-start.5 = (f32[2,256,512]{1,2,0:T(8,128)S(1)}, f32[2,256,512]{1,2,0:T(8,128)}, u32[]{:S(2)}) copy-start(f32[2,256,512]{1,2,0:T(8,128)} %copy.72) | copy-start | bytes 3145732
  434.9 4.1 copy-start.1
  451.8 60.6 %reduce-scatter.5.cloned.1.call-start = ((), (), s32[]{:S(2)}) async-start(), calls=%async_computation.8 | async-start | bytes 2293760 | tf_op jit(solution)/shard_map/reduce_scatter | solution.py:49
  453.3 80.1 %reduce-scatter.11.cloned.1.call-start = ((), (), s32[]{:S(2)}) async-start(), calls=%async_computation.11 | async-start | bytes 573440 | tf_op jit(solution)/shard_map/reduce_scatter | solution.py:49
  482.2 74.8 %reduce-scatter.7.cloned.1.call-start = ((), (), s32[]{:S(2)}) async-start(), calls=%async_computation.9 | async-start | bytes 573440 | tf_op jit(solution)/shard_map/reduce_scatter | solution.py:49
  512.4 100.5 %all-gather.5.cloned.1.call-start = ((), (), s32[]{:S(2)}) async-start(), calls=%async_computation.12 | async-start | bytes 7569408 | tf_op jit(solution)/shard_map/all_gather | solution.py:107
  612.9 8.3 %copy-start.2 = (bf16[3584,2,512]{2,0,1:T(8,128)(2,1)S(1)}, bf16[3584,2,512]{2,0,1:T(8,128)(2,1)}, u32[]{:S(2)}) copy-start(bf16[3584,2,512]{2,0,1:T(8,128)(2,1)} %all-gather.5.cloned.1.call-done) | copy-start | bytes 22020100
Sparse Core Ops, SparseCore 0:
  9.6 24.6 all-gather.2
  79.3 44.2 all-reduce.3
  125.9 46.9 all-reduce.5
  451.9 30.1 reduce-scatter.8
  485.0 27.3 reduce-scatter.4
  514.6 18.8 reduce-scatter.10
  535.9 21.0 reduce-scatter.6
  559.8 53.0 all-gather.4
